TPU v7x, 32 devices: a whole 2x2x4 slice. The times are simulated.
32 devices in a mesh: expert: 4 (over z), shard: 8 (over y, x, core).
Axes of the slice: x: 2, y: 2, z: 4, core: 2. Of those that a mesh axis runs over, the one named last changes fastest.
Arguments:
- master_gate: float32 [64, 2048, 1024], P('expert', 'shard'), may hold values from -0.1875 to 0.1875
- second_gate: float32 [64, 2048, 1024], P('expert', 'shard'), may hold values from -0.125 to 0.125
- master_up: float32 [64, 2048, 1024], P('expert', 'shard'), may hold values from -0.1875 to 0.1875
- second_up: float32 [64, 2048, 1024], P('expert', 'shard'), may hold values from -0.125 to 0.125
- mix_share: float32 [64], P('expert'), may hold values from 0.2 to 0.8
- router_weight: float32 [2048, 64], P('shard', 'expert'), may hold values from -0.125 to 0.125
- router_gain: float32 [2048], P('shard'), may hold values from 0.25 to 1.75
Outputs:
- final_gate: bfloat16 [64, 2048, 1024], P('expert', None, 'shard')
- final_up: bfloat16 [64, 2048, 1024], P('expert', None, 'shard')
- scale_gate: float32 [64, 1024], P('expert', 'shard')
- scale_up: float32 [64, 1024], P('expert', 'shard')
- serve_router: bfloat16 [2048, 64], replicated
All inputs are finite; a program needn't handle non-finite values.
Results may differ from a plain program's by a relative error of at most 0.001.
Values may be sent and summed in bfloat16 or wider, within the bound.
A program may use at most 256 MiB of HBM per device.

v0:
```python
import jax
import jax.numpy as jnp
from jax import lax
from jax.sharding import PartitionSpec as P

D_MODEL = 2048


def local(master_gate, second_gate, master_up, second_up, mix_share, router_weight, router_gain):
    merged_gate = (
        mix_share[:, None, None] * master_gate + (1.0 - mix_share[:, None, None]) * second_gate
    )
    merged_up = mix_share[:, None, None] * master_up + (1.0 - mix_share[:, None, None]) * second_up
    total_gate, total_up = lax.psum(
        (jnp.sum(jnp.abs(merged_gate), axis=1), jnp.sum(jnp.abs(merged_up), axis=1)), "shard"
    )
    scale_gate = total_gate / D_MODEL
    scale_up = total_up / D_MODEL
    narrow_gate, narrow_up = (
        (merged_gate / jnp.expand_dims(scale_gate, 1)).astype(jnp.bfloat16),
        (merged_up / jnp.expand_dims(scale_up, 1)).astype(jnp.bfloat16),
    )
    final_gate, final_up = (
        lax.all_to_all(narrow_gate, "shard", split_axis=2, concat_axis=1, tiled=True),
        lax.all_to_all(narrow_up, "shard", split_axis=2, concat_axis=1, tiled=True),
    )
    scale_gate = lax.dynamic_slice_in_dim(
        scale_gate, lax.axis_index("shard") * final_gate.shape[2], final_gate.shape[2], axis=1
    )
    scale_up = lax.dynamic_slice_in_dim(
        scale_up, lax.axis_index("shard") * final_up.shape[2], final_up.shape[2], axis=1
    )
    part_router = (router_weight * router_gain[:, None]).astype(jnp.bfloat16)
    row_router = lax.all_gather(part_router, "shard", axis=0, tiled=True)
    serve_router = lax.all_gather(row_router, "expert", axis=1, tiled=True)
    return (final_gate, final_up, scale_gate, scale_up, serve_router)


def solution(mesh):
    placed = (
        P("expert", "shard", None),
        P("expert", "shard", None),
        P("expert", "shard", None),
        P("expert", "shard", None),
        P("expert"),
        P("shard", "expert"),
        P("shard"),
    )
    return jax.shard_map(
        local,
        mesh=mesh,
        in_specs=placed,
        out_specs=(
            P("expert", None, "shard"),
            P("expert", None, "shard"),
            P("expert", "shard"),
            P("expert", "shard"),
            P(),
        ),
        check_vma=False,
    )
```

profile of v0, /device:TPU:0, one launch (start us, length us, event | category | flops | bytes accessed | tf_op | source)
XLA Modules:
  0.0 434.8 jit_solution(18230987575285412976)
XLA Ops:
  7.2 0.0 all-reduce.3.cloned.1.call-start
  7.2 17.6 %copy.22 = f32[16,256,1024]{1,0,2:T(8,128)} copy(f32[16,256,1024]{2,1,0:T(8,128)} %param.7) | data formatting | bytes 33554432 | tf_op args[0]
  24.8 17.6 %copy.23 = f32[16,256,1024]{1,0,2:T(8,128)} copy(f32[16,256,1024]{2,1,0:T(8,128)} %param.8) | data formatting | bytes 33554432 | tf_op args[1]
  42.4 17.6 %copy.25 = f32[16,256,1024]{1,0,2:T(8,128)} copy(f32[16,256,1024]{2,1,0:T(8,128)} %param.9) | data formatting | bytes 33554432 | tf_op args[2]
  60.0 0.0 copy-start.1
  60.0 17.6 %copy.26 = f32[16,256,1024]{1,0,2:T(8,128)} copy(f32[16,256,1024]{2,1,0:T(8,128)} %param.10) | data formatting | bytes 33554432 | tf_op args[3]
  77.6 0.0 copy-done.1
  77.6 23.7 %abs_reduce_fusion = (f32[16,1024]{0,1:T(8,128)}, f32[16,1024]{0,1:T(8,128)}) fusion(f32[16,256,1024]{1,0,2:T(8,128)} %copy.26, f32[16]{0:T(128)S(1)} %broadcast_subtract_fusion, f32[16,256,1024]{1,0,2:T(8,128)} %copy.25, f32[16]{0:T(128)S(1)} %copy-done.1, f32[16,256,1024]{1,0,2:T(8,128)} %copy.23, f32[16,256,1024]{1,0,2:T(8,128)} %copy.22), kind=kLoop, calls=%fused_computation.1 | loop fusion | flops 41910272 | bytes 67240064 | tf_op jit(solution)/shard_map/reduce_sum | solution.py:15
  101.3 0.0 all-reduce.3.cloned.1.call-update
  101.4 59.6 %all-reduce.3.cloned.1.call-done = (f32[16,1024]{0,1:T(8,128)}, f32[16,1024]{0,1:T(8,128)}) async-done(((f32[16,1024]{0,1:T(8,128)}, f32[16,1024]{0,1:T(8,128)}), (f32[16,1024]{0,1:T(8,128)}, f32[16,1024]{0,1:T(8,128)})) %all-reduce.3.cloned.1.call-update) | async-done | bytes 131088 | tf_op jit(solution)/shard_map/psum | solution.py:14
  161.0 1.3 broadcast_multiply_fusion
  162.3 25.3 %divide_convert_fusion = (bf16[16,256,1024]{1,0,2:T(8,128)(2,1)}, bf16[16,256,1024]{1,0,2:T(8,128)(2,1)S(1)}) fusion(f32[16,1024]{0,1:T(8,128)S(1)} %get-tuple-element.16, f32[16,256,1024]{1,0,2:T(8,128)} %copy.26, f32[16]{0:T(128)S(1)} %broadcast_subtract_fusion, f32[16,256,1024]{1,0,2:T(8,128)} %copy.25, f32[16]{0:T(128)S(1)} %copy-done.1, ...), kind=kLoop, calls=%fused_computation | loop fusion | flops 41943040 | bytes 84017280 | tf_op jit(solution)/shard_map/convert_element_type | solution.py:21
  187.6 0.0 copy-start
  187.6 0.0 copy-start.2
  187.6 97.6 %all_to_all.36 = bf16[16,256,1024]{1,0,2:T(8,128)(2,1)} all-to-all(bf16[16,256,1024]{1,0,2:T(8,128)(2,1)S(1)} %get-tuple-element.15), channel_id=1, replica_groups=mesh['expert'=4,'shard'=8] {'shard'}, dimensions={2} | all-to-all | bytes 16777216 | tf_op jit(solution)/shard_map/all_to_all | solution.py:24
  285.2 4.9 %all-to-all-start.1 = ((bf16[16,256,1024]{1,0,2:T(8,128)(2,1)}), bf16[16,256,1024]{1,0,2:T(8,128)(2,1)}, u32[]{:S(2)}, u32[]{:S(2)}) async-start(bf16[16,256,1024]{1,0,2:T(8,128)(2,1)} %get-tuple-element.14), calls=%async_computation.1 | async-start | bytes 16777216 | tf_op jit(solution)/shard_map/all_to_all | solution.py:25
  290.2 0.0 copy-done
  290.2 0.0 copy-done.2
  290.2 97.2 %all_gather.6 = bf16[2048,16]{0,1:T(8,128)(2,1)S(1)} all-gather(bf16[256,16]{0,1:T(8,128)(2,1)S(1)} %multiply_convert_fusion), channel_id=1, replica_groups=mesh['expert'=4,'shard'=8] {'shard'}, dimensions={0}, use_global_device_ids=true | all-gather | bytes 73728 | tf_op jit(solution)/shard_map/all_gather | solution.py:34
  387.4 14.0 %all_gather.7 = bf16[2048,64]{0,1:T(8,128)(2,1)S(1)} all-gather(bf16[2048,16]{0,1:T(8,128)(2,1)S(1)} %all_gather.6), channel_id=1, replica_groups=mesh['expert'=4,'shard'=8] {'expert'}, dimensions={1}, use_global_device_ids=true | all-gather | bytes 327680 | tf_op jit(solution)/shard_map/all_gather | solution.py:35
  401.3 0.7 copy.28
  402.0 0.7 copy.29
  402.7 12.3 %copy.24 = bf16[16,8,256,128]{3,2,1,0:T(8,128)(2,1)} copy(bf16[16,8,256,128]{2,0,3,1:T(8,128)(2,1)} %bitcast.8) | data formatting | bytes 16777216 | tf_op jit(solution)/shard_map/all_to_all | solution.py:24
  415.0 0.0 all-to-all-done.1
  415.0 12.3 %copy.27 = bf16[16,8,256,128]{3,2,1,0:T(8,128)(2,1)} copy(bf16[16,8,256,128]{2,0,3,1:T(8,128)(2,1)} %bitcast.4) | data formatting | bytes 16777216 | tf_op jit(solution)/shard_map/all_to_all | solution.py:25
  427.2 0.7 copy.33
  (4 shorter events, 0.0 us)
Async XLA Ops:
  7.2 153.8 %all-reduce.3.cloned.1.call-start = ((), (), s32[]{:S(2)}) async-start(), calls=%async_computation.2 | async-start | bytes 2097152 | tf_op jit(solution)/shard_map/psum | solution.py:14
  60.0 17.6 %copy-start.1 = (f32[16]{0:T(128)S(1)}, f32[16]{0:T(128)}, u32[]{:S(2)}) copy-start(f32[16]{0:T(128)} %param.11) | copy-start | bytes 196
  187.6 102.6 %copy-start = (f32[256,16]{0,1:T(8,128)S(1)}, f32[256,16]{0,1:T(8,128)}, u32[]{:S(2)}) copy-start(f32[256,16]{0,1:T(8,128)} %param.12) | copy-start | bytes 49156
  187.6 102.6 %copy-start.2 = (f32[256]{0:T(256)S(1)}, f32[256]{0:T(256)}, u32[]{:S(2)}) copy-start(f32[256]{0:T(256)} %param.13) | copy-start | bytes 3076
  285.2 129.8 %all-to-all-start.1 = ((bf16[16,256,1024]{1,0,2:T(8,128)(2,1)}), bf16[16,256,1024]{1,0,2:T(8,128)(2,1)}, u32[]{:S(2)}, u32[]{:S(2)}) async-start(bf16[16,256,1024]{1,0,2:T(8,128)(2,1)} %get-tuple-element.14), calls=%async_computation.1 | async-start | bytes 16777216 | tf_op jit(solution)/shard_map/all_to_all | solution.py:25
Sparse Core Ops, SparseCore 0:
  101.5 59.4 all-reduce.2
where the time goes:
time: 437 us; the launch traced here: 435 us
  blocking collectives  209 us (48%)
  local copies, waits for them, and re-layouts  97 us (22%)
  waiting for transfers between devices  59.7 us (14%)
  other arithmetic  50.3 us (12%)
  between operations  14.1 us (3%)
  starting transfers between devices  4.98 us (1%)
    all_to_all x1, blocking collectives, local(): lax.all_to_all(narrow_gate, 'shard', split_axis=2, concat_axis=1, tiled=T...  97.6 us
    all_gather x1, blocking collectives, local(): row_router = lax.all_gather(part_router, 'shard', axis=0, tiled=True)  97.2 us
    unnamed x13, local copies, waits for them, and re-layouts  72.5 us
    psum x1, waiting for transfers between devices, local(): lax.psum((jnp.sum(jnp.abs(merged_gate), axis=1), jnp.sum(jnp.abs(merged_u...  59.6 us
    convert_element_type x1, other arithmetic, local(): (merged_up / jnp.expand_dims(scale_up, 1)).astype(jnp.bfloat16)  25.3 us
    reduce_sum x1, other arithmetic, local(): jnp.sum(jnp.abs(merged_up), axis=1)  23.7 us
    all_gather x1, blocking collectives, local(): serve_router = lax.all_gather(row_router, 'expert', axis=1, tiled=True)  14 us
    all_to_all x1, local copies, waits for them, and re-layouts, local(): lax.all_to_all(narrow_up, 'shard', split_axis=2, concat_axis=1, tiled=True)  12.3 us
  transfers between devices with their start and end apart: 2, of which 1 were waited for; matrix products, arithmetic and copies ran while one was open for 3% of the time, Pallas kernels for 0%

commit v1 on v0

--- a/solution.py
+++ b/solution.py
@@ -21,7 +21,12 @@
         (merged_up / jnp.expand_dims(scale_up, 1)).astype(jnp.bfloat16),
     )
     final_gate, final_up = (
-        lax.all_to_all(narrow_gate, "shard", split_axis=2, concat_axis=1, tiled=True),
+        jnp.concatenate(
+            lax.all_to_all(
+                jnp.stack(jnp.split(narrow_gate, lax.axis_size("shard"), axis=2)), "shard", 0, 0
+            ),
+            axis=1,
+        ),
         lax.all_to_all(narrow_up, "shard", split_axis=2, concat_axis=1, tiled=True),
     )
     scale_gate = lax.dynamic_slice_in_dim(

time: 437 us -> 376 us (0.86)
  blocking collectives: 209 us -> 111 us
  waiting for transfers between devices: 59.7 us -> 135 us
  local copies, waits for them, and re-layouts: 97 us -> 49.8 us
  starting transfers between devices: 4.98 us -> 9.99 us
    all_to_all x1 -> x0, blocking collectives: 97.6 us -> none  [local(): lax.all_to_all(narrow_gate, 'shard', split_axis=2, concat_axis=1, tiled=T...]
    all_to_all x1, waiting for transfers between devices: 0.01 us -> 78.9 us  [local(): lax.all_to_all(narrow_up, 'shard', split_axis=2, concat_axis=1, tiled=True)]
    unnamed x13 -> x16, local copies, waits for them, and re-layouts: 72.5 us -> 14.6 us
    convert_element_type x0 -> x1, local copies, waits for them, and re-layouts: none -> 12.6 us  [local(): (merged_up / jnp.expand_dims(scale_up, 1)).astype(jnp.bfloat16)]
    all_to_all x0 -> x1, starting transfers between devices: none -> 5.02 us  [local(): lax.all_to_all(jnp.stack(jnp.split(narrow_gate, lax.axis_size('shard'), a...]
    all_to_all x1, local copies, waits for them, and re-layouts: 12.3 us -> 7.89 us  [local(): lax.all_to_all(jnp.stack(jnp.split(narrow_gate, lax.axis_size('shard'), a...]
  transfers between devices with their start and end apart: 2 -> 3, of which waited for: 1 -> 2; matrix products, arithmetic and copies ran while one was open for 3% -> 8% of each run, Pallas kernels for 0% -> 0%
where the time goes in v1:
time: 376 us; the launch traced here: 375 us
  waiting for transfers between devices  135 us (36%)
  blocking collectives  111 us (30%)
  other arithmetic  54.3 us (14%)
  local copies, waits for them, and re-layouts  49.8 us (13%)
  between operations  14.1 us (4%)
  starting transfers between devices  9.99 us (3%)
    all_gather x1, blocking collectives, local(): row_router = lax.all_gather(part_router, 'shard', axis=0, tiled=True)  97.2 us
    all_to_all x1, waiting for transfers between devices, local(): lax.all_to_all(narrow_up, 'shard', split_axis=2, concat_axis=1, tiled=True)  78.9 us
    psum x1, waiting for transfers between devices, local(): lax.psum((jnp.sum(jnp.abs(merged_gate), axis=1), jnp.sum(jnp.abs(merged_u...  56.4 us
    convert_element_type x1, other arithmetic, local(): (merged_up / jnp.expand_dims(scale_up, 1)).astype(jnp.bfloat16)  29.4 us
    reduce_sum x1, other arithmetic, local(): jnp.sum(jnp.abs(merged_up), axis=1)  23.3 us
    unnamed x16, local copies, waits for them, and re-layouts  14.6 us
    all_gather x1, blocking collectives, local(): serve_router = lax.all_gather(row_router, 'expert', axis=1, tiled=True)  14 us
    convert_element_type x1, local copies, waits for them, and re-layouts, local(): (merged_up / jnp.expand_dims(scale_up, 1)).astype(jnp.bfloat16)  12.6 us
  transfers between devices with their start and end apart: 3, of which 2 were waited for; matrix products, arithmetic and copies ran while one was open for 8% of the time, Pallas kernels for 0%

profile of v1, /device:TPU:0, one launch (start us, length us, event | category | flops | bytes accessed | tf_op | source)
XLA Modules:
  0.0 374.7 jit_solution(9546674227950947289)
XLA Ops:
  7.2 0.0 all-reduce.3.cloned.1.call-start
  7.2 0.7 broadcast_subtract_fusion
  7.9 0.0 copy-start.2
  7.9 23.3 %abs_reduce_fusion = (f32[16,1024]{1,0:T(8,128)}, f32[16,1024]{1,0:T(8,128)}) fusion(f32[16,256,1024]{2,1,0:T(8,128)} %param.10, f32[16]{0:T(128)S(1)} %broadcast_subtract_fusion, f32[16,256,1024]{2,1,0:T(8,128)} %param.9, f32[16]{0:T(128)} %param.11, f32[16,256,1024]{2,1,0:T(8,128)} %param.8, f32[16,256,1024]{2,1,0:T(8,128)} %param.7), kind=kLoop, calls=%fused_computation.1 | loop fusion | flops 41910272 | bytes 67240064 | tf_op jit(solution)/shard_map/reduce_sum | solution.py:15
  31.2 0.0 all-reduce.3.cloned.1.call-update
  31.2 56.4 %all-reduce.3.cloned.1.call-done = (f32[16,1024]{1,0:T(8,128)}, f32[16,1024]{1,0:T(8,128)}) async-done(((f32[16,1024]{1,0:T(8,128)}, f32[16,1024]{1,0:T(8,128)}), (f32[16,1024]{1,0:T(8,128)}, f32[16,1024]{1,0:T(8,128)})) %all-reduce.3.cloned.1.call-update) | async-done | bytes 131088 | tf_op jit(solution)/shard_map/psum | solution.py:14
  87.6 0.9 broadcast_multiply_fusion
  88.5 0.0 copy-done.2
  88.5 29.4 %divide_convert_fusion = (bf16[16,256,1024]{2,1,0:T(8,128)(2,1)}, bf16[16,256,1024]{2,1,0:T(8,128)(2,1)}) fusion(f32[16,1024]{1,0:T(8,128)S(1)} %get-tuple-element.11, f32[16,256,1024]{2,1,0:T(8,128)} %param.10, f32[16]{0:T(128)S(1)} %broadcast_subtract_fusion, f32[16,256,1024]{2,1,0:T(8,128)} %param.9, f32[16]{0:T(128)S(1)} %copy-done.2, ...), kind=kLoop, calls=%fused_computation | loop fusion | flops 41943040 | bytes 84017280 | tf_op jit(solution)/shard_map/convert_element_type | solution.py:21
  117.9 12.6 %copy.31 = bf16[16,256,1024]{1,0,2:T(8,128)(2,1)} copy(bf16[16,256,1024]{2,1,0:T(8,128)(2,1)} %get-tuple-element.9) | data formatting | bytes 16777216 | tf_op jit(solution)/shard_map/convert_element_type | solution.py:21
  130.5 4.9 %all-to-all-start.1 = ((bf16[16,256,1024]{1,0,2:T(8,128)(2,1)}), bf16[16,256,1024]{1,0,2:T(8,128)(2,1)}, u32[]{:S(2)}, u32[]{:S(2)}) async-start(bf16[16,256,1024]{1,0,2:T(8,128)(2,1)} %copy.31), calls=%async_computation.1 | async-start | bytes 16777216 | tf_op jit(solution)/shard_map/all_to_all | solution.py:30
  135.5 0.0 copy-start
  135.5 2.4 fusion.7
  137.9 3.0 fusion.6
  140.9 2.3 fusion.5
  143.2 2.3 fusion.4
  145.5 0.0 copy-done
  145.5 1.2 fusion.3
  146.8 1.3 fusion.2
  148.1 1.3 fusion.1
  149.3 1.3 fusion
  150.6 0.0 copy-start.1
  150.6 0.0 copy-start.3
  150.6 78.9 %all-to-all-done.1 = bf16[16,256,1024]{1,0,2:T(8,128)(2,1)} async-done(((bf16[16,256,1024]{1,0,2:T(8,128)(2,1)}), bf16[16,256,1024]{1,0,2:T(8,128)(2,1)}, u32[]{:S(2)}, u32[]{:S(2)}) %all-to-all-start.1) | async-done | bytes 8388640 | tf_op jit(solution)/shard_map/all_to_all | solution.py:30
  229.5 5.0 %all-to-all-start = ((bf16[8,16,256,128]{3,2,1,0:T(8,128)(2,1)}), bf16[8,16,256,128]{3,2,1,0:T(8,128)(2,1)}, u32[]{:S(2)}, u32[]{:S(2)}) async-start(bf16[8,16,256,128]{3,2,1,0:T(8,128)(2,1)} %fusion), calls=%async_computation | async-start | bytes 16777216 | tf_op jit(solution)/shard_map/all_to_all | solution.py:25
  234.5 0.0 copy-done.1
  234.5 0.0 copy-done.3
  234.6 97.2 %all_gather.6 = bf16[2048,16]{0,1:T(8,128)(2,1)S(1)} all-gather(bf16[256,16]{0,1:T(8,128)(2,1)S(1)} %multiply_convert_fusion), channel_id=1, replica_groups=mesh['expert'=4,'shard'=8] {'shard'}, dimensions={0}, use_global_device_ids=true | all-gather | bytes 73728 | tf_op jit(solution)/shard_map/all_gather | solution.py:39
  331.7 14.0 %all_gather.7 = bf16[2048,64]{0,1:T(8,128)(2,1)S(1)} all-gather(bf16[2048,16]{0,1:T(8,128)(2,1)S(1)} %all_gather.6), channel_id=1, replica_groups=mesh['expert'=4,'shard'=8] {'expert'}, dimensions={1}, use_global_device_ids=true | all-gather | bytes 327680 | tf_op jit(solution)/shard_map/all_gather | solution.py:40
  345.7 0.6 constant_dynamic-slice_fusion
  346.3 0.6 constant_dynamic-slice_fusion.1
  346.9 12.3 %copy.32 = bf16[16,8,256,128]{3,2,1,0:T(8,128)(2,1)} copy(bf16[16,8,256,128]{2,0,3,1:T(8,128)(2,1)} %bitcast.11) | data formatting | bytes 16777216 | tf_op jit(solution)/shard_map/all_to_all | solution.py:30
  359.2 0.0 all-to-all-done
  359.2 7.9 %copy.30 = bf16[8,16,256,128]{3,2,0,1:T(8,128)(2,1)} copy(bf16[8,16,256,128]{3,2,1,0:T(8,128)(2,1)} %all-to-all-done) | data formatting | bytes 16777216 | tf_op jit(solution)/shard_map/all_to_all | solution.py:25
  367.1 0.7 copy.43
  (1 shorter events, 0.0 us)
Async XLA Ops:
  7.2 80.5 %all-reduce.3.cloned.1.call-start = ((), (), s32[]{:S(2)}) async-start(), calls=%async_computation.2 | async-start | bytes 262144 | tf_op jit(solution)/shard_map/psum | solution.py:14
  7.9 80.7 %copy-start.2 = (f32[16]{0:T(128)S(1)}, f32[16]{0:T(128)}, u32[]{:S(2)}) copy-start(f32[16]{0:T(128)} %param.11) | copy-start | bytes 196
  130.5 99.0 %all-to-all-start.1 = ((bf16[16,256,1024]{1,0,2:T(8,128)(2,1)}), bf16[16,256,1024]{1,0,2:T(8,128)(2,1)}, u32[]{:S(2)}, u32[]{:S(2)}) async-start(bf16[16,256,1024]{1,0,2:T(8,128)(2,1)} %copy.31), calls=%async_computation.1 | async-start | bytes 16777216 | tf_op jit(solution)/shard_map/all_to_all | solution.py:30
  135.5 10.1 %copy-start = (bf16[16,256,1024]{2,1,0:T(8,128)(2,1)S(1)}, bf16[16,256,1024]{2,1,0:T(8,128)(2,1)}, u32[]{:S(2)}) copy-start(bf16[16,256,1024]{2,1,0:T(8,128)(2,1)} %get-tuple-element.10) | copy-start | bytes 25165828
  150.6 83.9 %copy-start.1 = (f32[256,16]{0,1:T(8,128)S(1)}, f32[256,16]{0,1:T(8,128)}, u32[]{:S(2)}) copy-start(f32[256,16]{0,1:T(8,128)} %param.12) | copy-start | bytes 49156
  150.6 83.9 %copy-start.3 = (f32[256]{0:T(256)S(1)}, f32[256]{0:T(256)}, u32[]{:S(2)}) copy-start(f32[256]{0:T(256)} %param.13) | copy-start | bytes 3076
  229.5 129.7 %all-to-all-start = ((bf16[8,16,256,128]{3,2,1,0:T(8,128)(2,1)}), bf16[8,16,256,128]{3,2,1,0:T(8,128)(2,1)}, u32[]{:S(2)}, u32[]{:S(2)}) async-start(bf16[8,16,256,128]{3,2,1,0:T(8,128)(2,1)} %fusion), calls=%async_computation | async-start | bytes 16777216 | tf_op jit(solution)/shard_map/all_to_all | solution.py:25
Sparse Core Ops, SparseCore 0:
  31.3 56.2 all-reduce.2
